TPU v7x, 16 devices: a whole 2x2x2 slice. The times are simulated.
16 devices in a mesh: data: 16 (over z, y, x, core).
Axes of the slice: x: 2, y: 2, z: 2, core: 2. Of those that a mesh axis runs over, the one named last changes fastest.
Arguments:
- inputs: bfloat16 [256, 8, 1152], P('data')
- out_grad: float32 [256, 8, 1152], P('data')
- w_fwd0: bfloat16 [2304, 4608], replicated
- b_fwd0: float32 [4608], replicated
- w_rev0: bfloat16 [2304, 4608], replicated
- b_rev0: float32 [4608], replicated
- w_upper: bfloat16 [2, 2304, 4608], replicated
- b_upper: float32 [2, 4608], replicated
Outputs:
- output 1: float32 [256, 8, 1152], P('data')
- output 2: float32 [2304, 4608], replicated
- output 3: float32 [4608], replicated
- output 4: float32 [2304, 4608], replicated
- output 5: float32 [4608], replicated
- output 6: float32 [2, 2304, 4608], replicated
- output 7: float32 [2, 4608], replicated
All inputs are finite; a program needn't handle non-finite values.
Results may differ from a plain program's by a relative error of at most 0.0139591.
Values are sent between devices in bfloat16 or wider.
A program may use at most 1 GiB of HBM per device.

v0:
```python
import jax
import jax.numpy as jnp
from jax import lax
from jax.sharding import PartitionSpec as P

DATA_AXIS = 'data'


def cell_forward(pre_seq, w_rec, bias_vec, backwards):
    hidden_size = w_rec.shape[0]

    def cell_step(carry_in, pre_t):
        h_prev, c_prev = carry_in
        z_all = pre_t + jnp.dot(h_prev, w_rec, preferred_element_type=jnp.float32) + bias_vec
        in_gate = jax.nn.sigmoid(z_all[:, :hidden_size])
        forget_gate = jax.nn.sigmoid(z_all[:, hidden_size:2 * hidden_size])
        cand_gate = jnp.tanh(z_all[:, 2 * hidden_size:3 * hidden_size])
        out_gate = jax.nn.sigmoid(z_all[:, 3 * hidden_size:])
        c_new = forget_gate * c_prev + in_gate * cand_gate
        h_new = out_gate * jnp.tanh(c_new)
        gate_all = jnp.concatenate([in_gate, forget_gate, cand_gate, out_gate], axis=-1)
        return (h_new.astype(jnp.bfloat16), c_new), (gate_all, c_prev, h_new)

    batch_rows = pre_seq.shape[1]
    init_carry = (jnp.zeros((batch_rows, hidden_size), jnp.bfloat16), jnp.zeros((batch_rows, hidden_size), jnp.float32))
    return lax.scan(cell_step, init_carry, pre_seq, reverse=backwards)[1]


def cell_backward(dh_seq, gate_seq, c_prevs, w_rec, backwards):
    hidden_size = w_rec.shape[0]

    def back_step(carry_in, step_in):
        dh_rec, dc_next, db_rows = carry_in
        dh_in, gate_all, c_prev = step_in
        in_gate = gate_all[:, :hidden_size]
        forget_gate = gate_all[:, hidden_size:2 * hidden_size]
        cand_gate = gate_all[:, 2 * hidden_size:3 * hidden_size]
        out_gate = gate_all[:, 3 * hidden_size:]
        tanh_c = jnp.tanh(forget_gate * c_prev + in_gate * cand_gate)
        dh_tot = dh_in + dh_rec
        dc_cur = dc_next + dh_tot * out_gate * (1.0 - tanh_c * tanh_c)
        dz_all = jnp.concatenate([
            dc_cur * cand_gate * in_gate * (1.0 - in_gate),
            dc_cur * c_prev * forget_gate * (1.0 - forget_gate),
            dc_cur * in_gate * (1.0 - cand_gate * cand_gate),
            dh_tot * tanh_c * out_gate * (1.0 - out_gate)], axis=-1)
        dz_bf = dz_all.astype(jnp.bfloat16)
        dh_back = jnp.einsum('bg,hg->bh', dz_bf, w_rec, preferred_element_type=jnp.float32)
        return (dh_back, dc_cur * forget_gate, db_rows + dz_all), dz_bf

    batch_rows = dh_seq.shape[1]
    init_carry = (jnp.zeros((batch_rows, hidden_size), jnp.float32), jnp.zeros((batch_rows, hidden_size), jnp.float32), jnp.zeros((batch_rows, 4 * hidden_size), jnp.float32))
    final_carry, dz_seq = lax.scan(back_step, init_carry, (dh_seq, gate_seq, c_prevs), reverse=not backwards)
    return dz_seq, jnp.sum(final_carry[2], axis=0)


def weight_grads(layer_x, x_form, h_bf, dz_seq, backwards):
    x_part = jnp.einsum(x_form, layer_x, dz_seq, preferred_element_type=jnp.float32)
    if backwards:
        h_part = jnp.einsum('tbh,tbg->hg', h_bf[1:], dz_seq[:-1], preferred_element_type=jnp.float32)
    else:
        h_part = jnp.einsum('tbh,tbg->hg', h_bf[:-1], dz_seq[1:], preferred_element_type=jnp.float32)
    return jnp.concatenate([x_part, h_part], axis=0)


def layer_forward(layer_x, x_form, w_cat, bias_vec, backwards):
    hidden_size = w_cat.shape[0] // 2
    pre_seq = jnp.einsum(x_form, layer_x, w_cat[:hidden_size], preferred_element_type=jnp.float32)
    return cell_forward(pre_seq, w_cat[hidden_size:], bias_vec, backwards)


def reduce_grads(dw_cat, db_sum):
    summed = lax.psum((dw_cat.astype(jnp.bfloat16), db_sum.astype(jnp.bfloat16)), DATA_AXIS)
    return summed[0].astype(jnp.float32), summed[1].astype(jnp.float32)


def step_grads(inputs, out_grad, w_fwd0, b_fwd0, w_rev0, b_rev0, w_upper, b_upper, finish):
    hidden_size = w_fwd0.shape[0] // 2
    gate_f, cprev_f, hseq_f = layer_forward(inputs, 'bth,hg->tbg', w_fwd0, b_fwd0, False)
    gate_r, cprev_r, hseq_r = layer_forward(inputs, 'bth,hg->tbg', w_rev0, b_rev0, True)
    layer_x = (hseq_f + hseq_r).astype(jnp.bfloat16)
    saved = []
    for layer_idx in range(w_upper.shape[0]):
        gate_seq, c_prevs, h_seq = layer_forward(layer_x, 'tbh,hg->tbg', w_upper[layer_idx], b_upper[layer_idx], False)
        h_bf = h_seq.astype(jnp.bfloat16)
        saved.append((layer_x, gate_seq, c_prevs, h_bf))
        layer_x = h_bf
    dh_seq = jnp.swapaxes(out_grad, 0, 1)
    dw_list = []
    db_list = []
    for layer_idx in reversed(range(w_upper.shape[0])):
        layer_in, gate_seq, c_prevs, h_bf = saved[layer_idx]
        w_cat = w_upper[layer_idx]
        dz_seq, db_sum = cell_backward(dh_seq, gate_seq, c_prevs, w_cat[hidden_size:], False)
        dw_cat, db_sum = finish(weight_grads(layer_in, 'tbh,tbg->hg', h_bf, dz_seq, False), db_sum)
        dw_list.append(dw_cat)
        db_list.append(db_sum)
        dh_seq = jnp.einsum('tbg,hg->tbh', dz_seq, w_cat[:hidden_size], preferred_element_type=jnp.float32)
    dz_f, db_f = cell_backward(dh_seq, gate_f, cprev_f, w_fwd0[hidden_size:], False)
    dz_r, db_r = cell_backward(dh_seq, gate_r, cprev_r, w_rev0[hidden_size:], True)
    dw_f, db_f = finish(weight_grads(inputs, 'bth,tbg->hg', hseq_f.astype(jnp.bfloat16), dz_f, False), db_f)
    dw_r, db_r = finish(weight_grads(inputs, 'bth,tbg->hg', hseq_r.astype(jnp.bfloat16), dz_r, True), db_r)
    in_grad = jnp.einsum('tbg,hg->bth', dz_f, w_fwd0[:hidden_size], preferred_element_type=jnp.float32) + jnp.einsum('tbg,hg->bth', dz_r, w_rev0[:hidden_size], preferred_element_type=jnp.float32)
    return (in_grad, dw_f, db_f, dw_r, db_r, jnp.stack(dw_list[::-1]), jnp.stack(db_list[::-1]))


def solution(mesh):
    def per_device(inputs, out_grad, w_fwd0, b_fwd0, w_rev0, b_rev0, w_upper, b_upper):
        return step_grads(inputs, out_grad, w_fwd0, b_fwd0, w_rev0, b_rev0, w_upper, b_upper, reduce_grads)
    return jax.shard_map(per_device, mesh=mesh,
                         in_specs=(P(DATA_AXIS), P(DATA_AXIS), P(), P(), P(), P(), P(), P()),
                         out_specs=(P(DATA_AXIS), P(), P(), P(), P(), P(), P()),
                         check_vma=False)
```

profile of v0, /device:TPU:0, one launch (start us, length us, event | category | flops | bytes accessed | tf_op | source)
XLA Modules:
  0.0 1567.9 jit_solution(13454064673869351980)
XLA Ops:
  7.3 11.2 slice.275
  18.5 7.3 fusion.130
  37.1 51.1 %while.160 = (s32[]{:T(128)}, bf16[16,1152]{1,0:T(8,128)(2,1)S(1)}, f32[16,1152]{1,0:T(8,128)S(1)}, f32[8,16,4608]{2,1,0:T(8,128)S(1)}, f32[8,16,1152]{2,1,0:T(8...) while((s32[]{:T(128)}, bf16[16,1152]{1,0:T(8,128)(2,1)S(1)}, ...), condition=%wide.region_1.2_spmd.clone, body=%wide.region_0.1_spmd.clone.sunk | while | flops 170717184 | bytes 13142656 | solution.py:26
  91.9 56.6 %while.161 = (s32[]{:T(128)}, bf16[16,1152]{1,0:T(8,128)(2,1)S(1)}, f32[16,1152]{1,0:T(8,128)S(1)}, f32[8,16,4608]{2,1,0:T(8,128)}, f32[8,16,1152]{2,1,0:T(8,128...) while((s32[]{:T(128)}, bf16[16,1152]{1,0:T(8,128)(2,1)S(1)}, ...), condition=%wide.region_3.4_spmd.clone, body=%wide.region_2.3_spmd.clone.sunk | while | flops 170717184 | bytes 13142168 | solution.py:26
  148.5 16.0 %slice_bitcast_fusion = (bf16[1152,4608]{1,0:T(8,128)(2,1)}, bf16[1152,4608]{1,0:T(8,128)(2,1)}) fusion(bf16[2,2304,4608]{2,1,0:T(8,128)(2,1)} %param.30), kind=kLoop, calls=%fused_computation.235 | loop fusion | bytes 42467328 | tf_op jit(solution)/shard_map/slice | solution.py:69
  164.7 7.2 fusion.112
  173.8 51.9 %while.162 = (s32[]{:T(128)}, bf16[16,1152]{1,0:T(8,128)(2,1)S(1)}, f32[16,1152]{1,0:T(8,128)S(1)}, f32[8,16,4608]{2,1,0:T(8,128)S(1)}, f32[8,16,1152]{2,1,0:T(8...) while((s32[]{:T(128)}, bf16[16,1152]{1,0:T(8,128)(2,1)S(1)}, ...), condition=%wide.region_5.6_spmd.clone, body=%wide.region_4.5_spmd.clone.sunk | while | flops 170717184 | bytes 13179532 | solution.py:26
  173.9 5.6 fusion.232
  212.8 5.6 fusion.232
  219.3 5.6 fusion.232
  225.7 7.3 fusion.108
  235.5 57.2 %while.163 = (s32[]{:T(128)}, bf16[16,1152]{1,0:T(8,128)(2,1)S(1)}, f32[16,1152]{1,0:T(8,128)S(1)}, f32[8,16,4608]{2,1,0:T(8,128)}, f32[8,16,1152]{2,1,0:T(8,128...) while((s32[]{:T(128)}, bf16[16,1152]{1,0:T(8,128)(2,1)S(1)}, ...), condition=%wide.region_7.8_spmd.clone, body=%wide.region_6.7_spmd.clone.sunk | while | flops 170717184 | bytes 13180040 | solution.py:26
  295.8 84.7 %while.164 = (s32[]{:T(128)}, f32[16,1152]{1,0:T(8,128)S(1)}, f32[16,1152]{1,0:T(8,128)S(1)}, f32[16,4608]{1,0:T(8,128)S(1)}, bf16[8,16,4608]{2,1,0:T(8,128)(2,1...) while((s32[]{:T(128)}, f32[16,1152]{1,0:T(8,128)S(1)}, ...), condition=%wide.region_9.10_spmd.clone, body=%wide.region_8.9_spmd.clone.sunk | while | flops 172007424 | bytes 14672028 | solution.py:53
  299.5 6.8 fusion.242
  310.1 6.8 fusion.242
  320.7 6.8 fusion.242
  331.3 6.8 fusion.242
  341.8 6.8 fusion.242
  352.4 6.8 fusion.242
  363.0 6.8 fusion.242
  373.6 6.8 fusion.242
  381.2 8.7 fusion.106
  391.0 77.1 %while.165 = (s32[]{:T(128)}, f32[16,1152]{1,0:T(8,128)S(1)}, f32[16,1152]{1,0:T(8,128)S(1)}, f32[16,4608]{1,0:T(8,128)S(1)}, bf16[8,16,4608]{2,1,0:T(8,128)(2,1...) while((s32[]{:T(128)}, f32[16,1152]{1,0:T(8,128)S(1)}, ...), condition=%wide.region_11.12_spmd.clone, body=%wide.region_10.11_spmd.clone.sunk | while | flops 172007424 | bytes 14672028 | solution.py:53
  393.7 6.8 fusion.245
  403.4 6.8 fusion.245
  413.0 6.8 fusion.245
  422.6 6.8 fusion.245
  432.3 6.8 fusion.245
  441.9 6.8 fusion.245
  451.5 6.8 fusion.245
  461.2 6.8 fusion.245
  468.1 7.9 fusion.110
  481.6 5.6 fusion.98
  492.9 79.3 %while.166 = (s32[]{:T(128)}, f32[16,1152]{1,0:T(8,128)S(1)}, f32[16,1152]{1,0:T(8,128)S(1)}, f32[16,4608]{1,0:T(8,128)S(1)}, bf16[8,16,4608]{2,1,0:T(8,128)(2,1...) while((s32[]{:T(128)}, f32[16,1152]{1,0:T(8,128)S(1)}, ...), condition=%wide.region_13.14_spmd.clone, body=%wide.region_12.13_spmd.clone.sunk | while | flops 172007424 | bytes 14672028 | solution.py:53
  496.1 6.8 fusion.248
  506.0 6.8 fusion.248
  515.9 6.8 fusion.248
  525.8 6.8 fusion.248
  535.6 6.8 fusion.248
  545.5 6.8 fusion.248
  555.4 6.8 fusion.248
  565.3 6.8 fusion.248
  572.9 6.6 fusion.100
  579.5 5.6 fusion.105
  585.2 79.0 %while.167 = (s32[]{:T(128)}, f32[16,1152]{1,0:T(8,128)S(1)}, f32[16,1152]{1,0:T(8,128)S(1)}, f32[16,4608]{1,0:T(8,128)S(1)}, bf16[8,16,4608]{2,1,0:T(8,128)(2,1...) while((s32[]{:T(128)}, f32[16,1152]{1,0:T(8,128)S(1)}, ...), condition=%wide.region_15.16_spmd.clone, body=%wide.region_14.15_spmd.clone.sunk | while | flops 172007424 | bytes 14672008 | solution.py:53
  588.2 6.8 fusion.251
  598.1 6.8 fusion.251
  608.0 6.8 fusion.251
  617.8 6.8 fusion.251
  627.7 6.8 fusion.251
  637.6 6.8 fusion.251
  647.5 6.8 fusion.251
  657.3 6.8 fusion.251
  664.2 6.8 fusion.101
  676.5 5.7 fusion.103
  682.2 29.6 %maximum_bitcast_fusion.4 = (bf16[1,2304,4608]{2,1,0:T(8,128)(2,1)}, bf16[1,2304,4608]{2,1,0:T(8,128)(2,1)}) fusion(bf16[1152,4608]{1,0:T(8,128)(2,1)} %fusion.102, bf16[1152,4608]{1,0:T(8,128)(2,1)} %fusion.98, bf16[1152,4608]{1,0:T(8,128)(2,1)} %fusion.103, bf16[1152,4608]{1,0:T(8,128)(2,1)} %fusion.99), kind=kLoop, calls=%fused_computation.207 | loop fusion | flops 84934656 | bytes 84934656 | tf_op jit(solution)/shard_map/stack | solution.py:104
  711.9 29.7 %pad_maximum_fusion.4 = (bf16[2304,4608]{1,0:T(8,128)(2,1)}, bf16[2304,4608]{1,0:T(8,128)(2,1)}) fusion(bf16[1152,4608]{1,0:T(8,128)(2,1)} %fusion.100, bf16[1152,4608]{1,0:T(8,128)(2,1)} %fusion.105, bf16[1152,4608]{1,0:T(8,128)(2,1)} %fusion.101, bf16[1152,4608]{1,0:T(8,128)(2,1)} %fusion.104), kind=kLoop, calls=%fused_computation.205 | loop fusion | flops 84934656 | bytes 84934656 | tf_op jit(solution)/shard_map/concatenate | solution.py:63
  742.8 37.1 %all-reduce = (bf16[4608]{0:T(1024)(128)(2,1)S(1)}, bf16[4608]{0:T(1024)(128)(2,1)S(1)}, bf16[1,4608]{1,0:T(2,128)(2,1)S(1)}, bf16[1,4608]{1,0:T(2,128)(2,1)S(1)}) all-reduce(bf16[4608]{0:T(1024)(128)(2,1)S(1)} %reduce_sum.36, bf16[4608]{0:T(1024)(128)(2,1)S(1)} %reduce_sum.37, ...), channel_id=1, replica_groups=mesh['data'=16] {'data'}, use_global_device_ids=true, to_apply=%region_18.19 | all-reduce | flops 18432 | bytes 73728 | tf_op jit(solution)/shard_map/psum | solution.py:73
  781.2 7.5 fusion.114
  788.7 7.4 fusion.139
  797.8 680.5 %all-reduce.4.cloned.1.call-done = (bf16[2304,4608]{1,0:T(8,128)(2,1)}, bf16[2304,4608]{1,0:T(8,128)(2,1)}, bf16[1,2304,4608]{2,1,0:T(8,128)(2,1)}, bf16[1,2304,4608]{2,1,0:T(8,128)(2,1)}) async-done(((bf16[2304,4608]{1,0:T(8,128)(2,1)}, bf16[2304,4608]{1,0:T(8,128)(2,1)}, bf16[1,2304,4608]{2,1,0:T(8,128)(2,1)}, bf16[1,2304,4608]{2,1,0:T(8,128)(2,1)}), (bf16[2304,4608]{1,0:T(8,128)(2,1)}, ...) | async-done | bytes 84934672 | tf_op jit(solution)/shard_map/psum | solution.py:73
  1478.3 23.3 %convert_element_type.144 = f32[2304,4608]{1,0:T(8,128)} convert(bf16[2304,4608]{1,0:T(8,128)(2,1)} %get-tuple-element.1338) | non-fusion elementwise | flops 10616832 | bytes 63700992 | tf_op jit(solution)/shard_map/convert_element_type | solution.py:74
  1506.3 14.1 convert_element_type.148
  1520.4 40.1 %maximum_convert_fusion = f32[2,2304,4608]{2,1,0:T(8,128)} fusion(bf16[1,2304,4608]{2,1,0:T(8,128)(2,1)} %get-tuple-element.1340, bf16[1,2304,4608]{2,1,0:T(8,128)(2,1)} %get-tuple-element.1341), kind=kLoop, calls=%fused_computation.196 | loop fusion | flops 42467328 | bytes 127401984 | tf_op jit(solution)/shard_map/stack | solution.py:104
  (430 shorter events, 350.0 us)
Async XLA Ops:
  7.2 11.3 copy-start
  7.2 1471.1 %all-reduce.4.cloned.1.call-start = ((), (), s32[]{:S(2)}) async-start(), calls=%async_computation | async-start | bytes 169869312 | tf_op jit(solution)/shard_map/psum | solution.py:73
  7.2 18.6 %slice-start = ((s8[21233664]{0:T(1024)(128)(4,1)}), s8[4194304]{0:T(1024)(128)(4,1)S(1)}, s32[]{:S(2)}) async-start(s8[21233664]{0:T(1024)(128)(4,1)} %bitcast.337), calls=%async_computation.1 | async-start | bytes 8388608
  7.3 18.6 %slice-start.1 = ((s8[21233664]{0:T(1024)(128)(4,1)}), s8[4194304]{0:T(1024)(128)(4,1)S(1)}, s32[]{:S(2)}) async-start(s8[21233664]{0:T(1024)(128)(4,1)} %bitcast.337), calls=%async_computation.2 | async-start | bytes 8388608
  18.5 7.3 slice-start.2
  18.5 7.3 slice-start.3
  18.5 8.5 slice-start.4
  18.5 8.5 slice-start.5
  31.4 5.7 copy-start.24
  37.1 54.8 %copy-start.25 = (f32[4608]{0:T(1024)S(1)}, f32[4608]{0:T(1024)}, u32[]{:S(2)}) copy-start(f32[4608]{0:T(1024)} %param.29) | copy-start | bytes 55300
  88.3 3.6 copy-start.13
  148.5 16.0 %copy-start.14 = (f32[8,16,1152]{2,1,0:T(8,128)S(1)}, f32[8,16,1152]{2,1,0:T(8,128)}, u32[]{:S(2)}) copy-start(f32[8,16,1152]{2,1,0:T(8,128)} %get-tuple-element.923) | copy-start | bytes 1769476
  148.5 16.0 %copy-start.15 = (f32[8,16,1152]{2,1,0:T(8,128)S(1)}, f32[8,16,1152]{2,1,0:T(8,128)}, u32[]{:S(2)}) copy-start(f32[8,16,1152]{2,1,0:T(8,128)} %get-tuple-element.924) | copy-start | bytes 1769476
  164.6 7.4 copy-start.22
  164.7 8.0 copy-start.27
  164.7 8.0 copy-start.29
  380.4 0.7 copy-start.9
  381.2 9.8 copy-start.6
  381.2 9.8 copy-start.18
  468.0 13.6 copy-start.7
  468.0 8.0 copy-start.21
  468.0 8.0 copy-start.26
  476.0 5.6 copy-start.28
  481.6 5.6 copy-start.19
  487.2 5.6 copy-start.3
  487.2 5.7 copy-start.17
  572.1 0.7 copy-start.4
  572.1 7.3 copy-start.11
  579.5 5.7 copy-start.2
  579.5 5.7 copy-start.16
  671.0 5.6 copy-start.20
  671.0 5.6 copy-start.23
  741.6 1.0 copy-start.8
  741.6 1.0 copy-start.10
  741.6 1.1 copy-start.5
  781.2 7.5 copy-start.12
  1478.3 28.0 %copy-start.1 = (bf16[2304,4608]{1,0:T(8,128)(2,1)S(1)}, bf16[2304,4608]{1,0:T(8,128)(2,1)}, u32[]{:S(2)}) copy-start(bf16[2304,4608]{1,0:T(8,128)(2,1)} %get-tuple-element.1339) | copy-start | bytes 63700996
Sparse Core Ops, SparseCore 0:
  741.8 736.4 all-reduce.3
where the time goes:
time: 1580 us; the launch traced here: 1570 us
  waiting for transfers between devices  680 us (43%)
  matrix products  499 us (32%)
  other arithmetic  255 us (16%)
  local copies, waits for them, and re-layouts  79.8 us (5%)
  blocking collectives  37.1 us (2%)
    psum x1, waiting for transfers between devices, reduce_grads(): lax.psum((dw_cat.astype(jnp.bfloat16), db_sum.astype(jnp.bfloat16)), DATA...  680 us
    dot_general x32, matrix products, back_step(): jnp.einsum('bg,hg->bh', dz_bf, w_rec, preferred_element_type=jnp.float32)  219 us
    dot_general x32, matrix products, cell_step(): jnp.dot(h_prev, w_rec, preferred_element_type=jnp.float32)  177 us
    another operation x2, other arithmetic, step_grads(): jnp.stack(dw_list[::-1])  69.8 us
    concatenate x64, other arithmetic, back_step(): jnp.concatenate([dc_cur * cand_gate * in_gate * (1.0 - in_gate), dc_cur *...  61.7 us
    convert_element_type x4, other arithmetic, reduce_grads(): return (summed[0].astype(jnp.float32), summed[1].astype(jnp.float32))  38.6 us
    psum x1, blocking collectives, reduce_grads(): lax.psum((dw_cat.astype(jnp.bfloat16), db_sum.astype(jnp.bfloat16)), DATA...  37.1 us
    dynamic_update_slice x64, other arithmetic, cell_forward(): return lax.scan(cell_step, init_carry, pre_seq, reverse=backwards)[1]  35.8 us
  transfers between devices with their start and end apart: 1, of which 1 were waited for; matrix products, arithmetic and copies ran while one was open for 1% of the time, Pallas kernels for 0%

commit v1 on v0

v1 whole, which is shorter than its diff:
```python
import functools

import jax
import jax.numpy as jnp
from jax import lax
from jax.experimental import pallas as pl
from jax.experimental.pallas import tpu as pltpu
from jax.sharding import PartitionSpec as P

DATA_AXIS = 'data'
F32 = jnp.float32
BF16 = jnp.bfloat16
VMEM_LIMIT = 60 * 1024 * 1024


def dot_nt(lhs, rhs):
    return lax.dot_general(lhs, rhs, (((1,), (1,)), ((), ())), preferred_element_type=F32)


class Exchange:
    def __init__(self, ref, sems):
        self.ref, self.sems = ref, sems
        self.third = ref.shape[2] // 3
        self.me = lax.axis_index(DATA_AXIS)
        self.started = []

    def flip(self, dev, bit):
        return dev + bit * (1 - 2 * ((dev // bit) % 2))

    def bits(self, part):
        return [2 << ((part + r) % 3) for r in range(3)]

    def copies(self, part, rnd):
        bits = self.bits(part)
        peer = self.flip(self.me, bits[rnd])
        out = []
        for j in range(1 << rnd):
            blk, got = self.me, peer
            for k in range(rnd):
                if (j >> k) & 1:
                    blk, got = self.flip(blk, bits[k]), self.flip(got, bits[k])
            out.append((blk, got, peer, part * 7 + (1 << rnd) - 1 + j))
        return out

    def remote(self, blk, cols, peer, slot):
        view = self.ref.at[blk, :, cols]
        return pltpu.make_async_remote_copy(
            src_ref=view, dst_ref=view, send_sem=self.sems.at[0, slot], recv_sem=self.sems.at[1, slot],
            device_id=(peer,), device_id_type=pl.DeviceIdType.MESH)

    def cols(self, part):
        return pl.ds(part * self.third, self.third)

    def each(self, rnd):
        for part in range(3):
            for blk, got, peer, slot in self.copies(part, rnd):
                yield part, blk, got, peer, slot

    def send(self, rnd):
        for part, blk, got, peer, slot in self.each(rnd):
            self.remote(blk, self.cols(part), peer, slot).start()

    def wait(self, rnd):
        for part, blk, got, peer, slot in self.each(rnd):
            self.remote(blk, self.cols(part), peer, slot).wait()

    def own(self):
        return self.remote(self.me, pl.ds(0, 3 * self.third), self.flip(self.me, 1), 21)

    def share(self, rnd, start):
        for part, blk, got, peer, slot in self.each(rnd):
            copy = self.remote(got, self.cols(part), self.flip(self.me, 1), 22 + slot)
            if start:
                copy.start()
            else:
                copy.wait()


SLOTS = 43


def run_stage(ex, stage, open_ops):
    if stage > 0:
        if ('round', stage - 1) in open_ops:
            ex.wait(stage - 1)
            open_ops.remove(('round', stage - 1))
        ex.share(stage - 1, True)
        open_ops.append(('share', stage - 1))
    else:
        ex.own().start()
        open_ops.append(('own', 0))
    if stage < 3:
        ex.send(stage)
        open_ops.append(('round', stage))


class Comm:
    def __init__(self, plan, refs, sems, local_sems, sources):
        self.plan = plan
        self.exs = [Exchange(ref, sems.at[n]) for n, ref in enumerate(refs)]
        self.open_ops = [[] for _ in plan]
        self.local = [None if src is None else pltpu.make_async_copy(src, ex.ref.at[ex.me], local_sems.at[n])
                      for n, (src, ex) in enumerate(zip(sources, self.exs))]

    def begin(self):
        if not self.plan:
            return
        for copy in self.local:
            if copy is not None:
                copy.start()
        barrier = pltpu.get_barrier_semaphore()
        ex = self.exs[0]
        for bit in (1, 2, 4, 8):
            pl.semaphore_signal(barrier, inc=1, device_id=(ex.flip(ex.me, bit),),
                                device_id_type=pl.DeviceIdType.MESH)
        pl.semaphore_wait(barrier, 4)
        for copy in self.local:
            if copy is not None:
                copy.wait()
        self.at('start')

    def at(self, point):
        for ex, plan, ops in zip(self.exs, self.plan, self.open_ops):
            for stage in plan.get(point, ()):
                run_stage(ex, stage, ops)

    def in_loop(self, idx):
        points = sorted({p for plan in self.plan for p in plan if isinstance(p, int)})
        for point in points:
            pl.when(idx == point)(functools.partial(self.at, point))

    def finish(self):
        self.at('end')
        for ex, ops in zip(self.exs, self.open_ops):
            for kind, rnd in ops:
                if kind == 'round':
                    ex.wait(rnd)
                elif kind == 'share':
                    ex.share(rnd, False)
                else:
                    ex.own().wait()


def fwd_kernel(layer, steps, backwards, with_sum, plan, sources, *refs):
    refs = list(refs)
    x_ref, w_hbm, b_ref = refs[:3]
    refs = refs[3:]
    other_ref = refs.pop(0) if with_sum else None
    srcs = [x_ref if s == 'x' else refs.pop(0) if s == 'arg' else None for s in sources]
    refs = refs[sum(s == 'alias' for s in sources):]
    gate_ref, cprev_ref, h_ref, hbf_ref = refs[:4]
    refs = refs[4:]
    sum_ref = refs.pop(0) if with_sum else None
    g_refs = [refs.pop(0) for _ in plan]
    w_buf, pre, sems = refs[:3]
    comm = Comm(plan, g_refs, *(refs[3:5] if plan else (None, None)), srcs)
    hid = x_ref.shape[1]
    rows = x_ref.shape[0] // steps
    w_src = w_hbm if layer is None else w_hbm.at[layer]

    def w_copy(part, gate):
        at = (pl.ds(part * hid, hid), pl.ds(gate * hid, hid))
        return pltpu.make_async_copy(w_src.at[at], w_buf.at[at], sems.at[part * 4 + gate])

    for part in range(2):
        for gate in range(4):
            w_copy(part, gate).start()
    comm.begin()
    for gate in range(4):
        w_copy(0, gate).wait()
        cols = pl.ds(gate * hid, hid)
        pre[:, cols] = jnp.dot(x_ref[...], w_buf[:hid, cols], preferred_element_type=F32) + b_ref[:, cols]

    def cell(t, z_all, c_prev):
        in_gate = jax.nn.sigmoid(z_all[:, :hid])
        forget_gate = jax.nn.sigmoid(z_all[:, hid:2 * hid])
        cand_gate = jnp.tanh(z_all[:, 2 * hid:3 * hid])
        out_gate = jax.nn.sigmoid(z_all[:, 3 * hid:])
        c_new = forget_gate * c_prev + in_gate * cand_gate
        h_new = out_gate * jnp.tanh(c_new)
        gate_ref[t, :, :hid] = in_gate
        gate_ref[t, :, hid:2 * hid] = forget_gate
        gate_ref[t, :, 2 * hid:3 * hid] = cand_gate
        gate_ref[t, :, 3 * hid:] = out_gate
        cprev_ref[t] = c_prev
        h_ref[t] = h_new
        h_bf = h_new.astype(BF16)
        at = pl.ds(t * rows, rows) if isinstance(t, int) else pl.ds(pl.multiple_of(t * rows, rows), rows)
        hbf_ref[at, :] = h_bf
        if with_sum:
            sum_ref[at, :] = (other_ref[t] + h_new).astype(BF16)
        return h_bf, c_new

    first = steps - 1 if backwards else 0
    carry = cell(first, pre[first * rows:(first + 1) * rows, :], jnp.zeros((rows, hid), F32))
    for gate in range(4):
        w_copy(1, gate).wait()

    def step(idx, carry):
        h_bf, c_prev = carry
        comm.in_loop(idx)
        t = steps - 1 - idx if backwards else idx
        z_all = pre[pl.ds(pl.multiple_of(t * rows, rows), rows), :] + jnp.dot(
            h_bf, w_buf[hid:, :], preferred_element_type=F32)
        return cell(t, z_all, c_prev)

    lax.fori_loop(1, steps, step, carry)
    comm.finish()


def call(kernel, name, args, n_vmem, outs, scratch, plan, blocks, aliases, collective, flops):
    vm, hbm = pl.BlockSpec(memory_space=pltpu.VMEM), pl.BlockSpec(memory_space=pl.ANY)
    in_specs = [hbm if n == 1 or n >= n_vmem else vm for n in range(len(args))]
    out_specs = [vm] * len(outs) + [hbm] * len(blocks)
    params = dict(vmem_limit_bytes=VMEM_LIMIT)
    if plan:
        params.update(collective_id=collective, has_side_effects=True)
        scratch = scratch + [pltpu.SemaphoreType.DMA((len(plan), 2, SLOTS)), pltpu.SemaphoreType.DMA((len(plan),))]
    return pl.pallas_call(
        kernel,
        out_shape=outs + [jax.ShapeDtypeStruct(shape, BF16) for shape in blocks],
        in_specs=in_specs,
        out_specs=out_specs,
        scratch_shapes=scratch,
        input_output_aliases=aliases,
        compiler_params=pltpu.CompilerParams(**params),
        cost_estimate=pl.CostEstimate(flops=flops, bytes_accessed=40 << 20, transcendentals=0),
        name=name,
    )(*args)


def gather_args(args, gathers, n_outs, x_rows):
    args += [blk for kind, blk, _ in gathers if kind == 'arg']
    n_vmem = len(args)
    aliases = {}
    blocks = []
    devs = lax.axis_size(DATA_AXIS)
    for n, (kind, blk, _) in enumerate(gathers):
        if kind == 'alias':
            aliases[len(args)] = n_outs + n
            args.append(blk)
            blocks.append(blk.shape)
        else:
            blocks.append((devs,) + (x_rows if kind == 'x' else blk).shape)
    return [p for _, _, p in gathers], [kind for kind, _, _ in gathers], blocks, n_vmem, aliases


def lstm_forward(x_rows, w_cat, layer, bias_row, steps, backwards, collective, other=None, gathers=()):
    hid = x_rows.shape[1]
    rows = x_rows.shape[0] // steps
    with_sum = other is not None
    outs = [jax.ShapeDtypeStruct((steps, rows, 4 * hid), F32),
            jax.ShapeDtypeStruct((steps, rows, hid), F32),
            jax.ShapeDtypeStruct((steps, rows, hid), F32),
            jax.ShapeDtypeStruct((steps * rows, hid), BF16)]
    args = [x_rows, w_cat, bias_row]
    if with_sum:
        outs.append(jax.ShapeDtypeStruct((steps * rows, hid), BF16))
        args.append(other)
    plan, sources, blocks, n_vmem, aliases = gather_args(args, gathers, len(outs), x_rows)
    return call(functools.partial(fwd_kernel, layer, steps, backwards, with_sum, plan, sources), 'lstm_fwd', args,
                n_vmem, outs,
                [pltpu.VMEM((2 * hid, 4 * hid), BF16), pltpu.VMEM((steps * rows, 4 * hid), F32),
                 pltpu.SemaphoreType.DMA((8,))],
                plan, blocks, aliases, collective, 4 * steps * rows * hid * 4 * hid * 8)


def bwd_kernel(layer, steps, backwards, with_sum, plan, sources, *refs):
    refs = list(refs)
    dh_ref, w_hbm, gate_ref, cprev_ref = refs[:4]
    refs = refs[4:]
    other_ref = refs.pop(0) if with_sum else None
    srcs = [refs.pop(0) if s == 'arg' else None for s in sources]
    refs = refs[sum(s == 'alias' for s in sources):]
    dz_ref, db_ref, dx_ref = refs[:3]
    refs = refs[3:]
    g_refs = [refs.pop(0) for _ in plan]
    w_buf, sems = refs[:2]
    comm = Comm(plan, g_refs, *(refs[2:4] if plan else (None, None)), srcs)
    rows, hid = dh_ref.shape[1:]
    w_src = w_hbm if layer is None else w_hbm.at[layer]

    def w_copy(part):
        at = pl.ds(part * hid, hid)
        return pltpu.make_async_copy(w_src.at[at], w_buf.at[at], sems.at[part])

    w_copy(1).start()
    w_copy(0).start()
    comm.begin()

    def cell(t, dh_rec, dc_next):
        in_gate = gate_ref[t, :, :hid]
        forget_gate = gate_ref[t, :, hid:2 * hid]
        cand_gate = gate_ref[t, :, 2 * hid:3 * hid]
        out_gate = gate_ref[t, :, 3 * hid:]
        c_prev = cprev_ref[t]
        tanh_c = jnp.tanh(forget_gate * c_prev + in_gate * cand_gate)
        dh_tot = dh_ref[t] + dh_rec
        dc_cur = dc_next + dh_tot * out_gate * (1.0 - tanh_c * tanh_c)
        parts = [dc_cur * cand_gate * in_gate * (1.0 - in_gate),
                 dc_cur * c_prev * forget_gate * (1.0 - forget_gate),
                 dc_cur * in_gate * (1.0 - cand_gate * cand_gate),
                 dh_tot * tanh_c * out_gate * (1.0 - out_gate)]
        at = pl.ds(pl.multiple_of(t * rows, rows), rows)
        for gate, part in enumerate(parts):
            cols = slice(gate * hid, (gate + 1) * hid)
            dz_ref[at, cols] = part.astype(BF16)
            db_ref[:, cols] += part[:8] + part[8:]
        return dc_cur * forget_gate

    db_ref[...] = jnp.zeros_like(db_ref)
    first = 0 if backwards else steps - 1
    zero = jnp.zeros((rows, hid), F32)
    dc = cell(first, zero, zero)
    w_copy(1).wait()

    def step(idx, dc_next):
        comm.in_loop(idx)
        prev = idx - 1 if backwards else steps - idx
        t = idx if backwards else steps - 1 - idx
        at = pl.ds(pl.multiple_of(prev * rows, rows), rows)
        dh_rec = dot_nt(dz_ref[at, :], w_buf[hid:, :])
        return cell(t, dh_rec, dc_next)

    lax.fori_loop(1, steps, step, dc)
    w_copy(0).wait()
    dx = dot_nt(dz_ref[...], w_buf[:hid, :])
    if with_sum:
        dx = dx + other_ref[...]
    dx_ref[...] = dx
    comm.finish()


def lstm_backward(dh_seq, w_cat, layer, gate_seq, c_prevs, backwards, collective, other=None, gathers=()):
    steps, rows, hid = dh_seq.shape
    with_sum = other is not None
    args = [dh_seq, w_cat, gate_seq, c_prevs] + ([other] if with_sum else [])
    plan, sources, blocks, n_vmem, aliases = gather_args(args, gathers, 3, None)
    return call(functools.partial(bwd_kernel, layer, steps, backwards, with_sum, plan, sources), 'lstm_bwd', args,
                n_vmem,
                [jax.ShapeDtypeStruct((steps * rows, 4 * hid), BF16),
                 jax.ShapeDtypeStruct((8, 4 * hid), F32),
                 jax.ShapeDtypeStruct((steps * rows, hid), F32)],
                [pltpu.VMEM((2 * hid, 4 * hid), BF16), pltpu.SemaphoreType.DMA((2,))],
                plan, blocks, aliases, collective, 4 * steps * rows * hid * 4 * hid * 12)


def dw_kernel(backwards, steps, rows, x_ref, h_ref, dz_ref, *refs):
    out_ref, shifted, turned = refs[-3:]
    part, col = pl.program_id(0), pl.program_id(1)
    span = steps * rows
    devs = x_ref.shape[0] // span

    def turn(src):
        for n in range(devs):
            at = slice(n * span, (n + 1) * span)
            turned[:, at] = src[at, :].T

    @pl.when((part == 0) & (col == 0))
    def _():
        turn(x_ref)

    @pl.when((part == 1) & (col == 0))
    def _():
        none = jnp.zeros((rows, h_ref.shape[1]), BF16)
        for n in range(devs):
            lo, hi = n * span, (n + 1) * span
            if backwards:
                shifted[lo:hi - rows, :] = h_ref[lo + rows:hi, :]
                shifted[hi - rows:hi, :] = none
            else:
                shifted[lo + rows:hi, :] = h_ref[lo:hi - rows, :]
                shifted[lo:lo + rows, :] = none
        turn(shifted)

    out_ref[...] = jnp.dot(turned[...], dz_ref[...], preferred_element_type=F32)


def weight_grad(x_all, h_all, dz_all, backwards, steps, planes=None, plane=None, into=None):
    devs, span, hid = x_all.shape
    count = devs * span
    wide = dz_all.shape[2]
    width = 512
    flat = lambda a: a.reshape(count, a.shape[-1])
    args = [flat(x_all), flat(h_all), flat(dz_all)]
    whole = pl.BlockSpec((count, hid), lambda p, n: (0, 0), pipeline_mode=pl.Buffered(1))
    in_specs = [whole, whole, pl.BlockSpec((count, width), lambda p, n: (0, n))]
    aliases = {}
    if into is not None:
        args.append(into)
        in_specs.append(pl.BlockSpec(memory_space=pl.ANY))
        aliases = {3: 0}
    if planes is None:
        out = jax.ShapeDtypeStruct((2 * hid, wide), F32)
        out_spec = pl.BlockSpec((hid, width), lambda p, n: (p, n))
    else:
        out = jax.ShapeDtypeStruct((planes, 2 * hid, wide), F32)
        out_spec = pl.BlockSpec((None, hid, width), lambda p, n: (plane, p, n))
    return pl.pallas_call(
        functools.partial(dw_kernel, backwards, steps, span // steps),
        grid=(2, wide // width),
        out_shape=out,
        in_specs=in_specs,
        out_specs=out_spec,
        scratch_shapes=[pltpu.VMEM((count, hid), BF16), pltpu.VMEM((hid, count), BF16)],
        input_output_aliases=aliases,
        compiler_params=pltpu.CompilerParams(vmem_limit_bytes=VMEM_LIMIT,
                                             dimension_semantics=('arbitrary', 'arbitrary')),
        cost_estimate=pl.CostEstimate(flops=4 * count * hid * wide, bytes_accessed=90 << 20, transcendentals=0),
        name='dw',
    )(*args)


def gather(rows):
    return lax.all_gather(rows, DATA_AXIS, axis=0)


def step_grads(inputs, out_grad, w_fwd0, b_fwd0, w_rev0, b_rev0, w_upper, b_upper):
    batch, steps, hid = inputs.shape
    seq = lambda a: a.reshape(steps, batch, a.shape[-1])
    row = lambda b: b[None, :]
    x_rows = jnp.swapaxes(inputs, 0, 1).reshape(steps * batch, hid)
    head, tail, last = {'start': (0,), 4: (1,)}, {'start': (2,)}, {'start': (3,)}
    gate_f, cprev_f, h_f, hb_f, all_x = lstm_forward(
        x_rows, w_fwd0, None, row(b_fwd0), steps, False, 0, gathers=(('x', None, head),))
    gate_r, cprev_r, h_r, hb_r, x1, all_x, all_f = lstm_forward(
        x_rows, w_rev0, None, row(b_rev0), steps, True, 1, h_f, gathers=(('alias', all_x, tail), ('arg', hb_f, head)))
    gate_1, cprev_1, _, hb_1, all_x, all_f, all_r, all_x1 = lstm_forward(
        x1, w_upper, 0, row(b_upper[0]), steps, False, 2,
        gathers=(('alias', all_x, last), ('alias', all_f, tail), ('arg', hb_r, head), ('x', None, head)))
    gate_2, cprev_2, _, hb_2, all_f, all_r, all_x1, all_1 = lstm_forward(
        hb_1, w_upper, 1, row(b_upper[1]), steps, False, 3,
        gathers=(('alias', all_f, last), ('alias', all_r, tail), ('alias', all_x1, tail), ('x', None, head)))

    dz_2, db_2, dx_2, all_r, all_x1, all_1, all_2 = lstm_backward(
        jnp.swapaxes(out_grad, 0, 1), w_upper, 1, gate_2, cprev_2, False, 4,
        gathers=(('alias', all_r, last), ('alias', all_x1, last), ('alias', all_1, tail),
                 ('arg', hb_2, {'start': (0,), 2: (1,), 5: (2,)})))
    dz_1, db_1, dx_1, all_1, all_2, dz2_all = lstm_backward(
        seq(dx_2), w_upper, 0, gate_1, cprev_1, False, 5,
        gathers=(('alias', all_1, last), ('alias', all_2, last), ('arg', dz_2, {'start': (0,), 3: (1,)})))
    dz_f, db_f, dx_f, dz2_all, dz1_all = lstm_backward(
        seq(dx_1), w_fwd0, None, gate_f, cprev_f, False, 6,
        gathers=(('alias', dz2_all, {'start': (2,)}), ('arg', dz_1, {'start': (0,), 5: (1,)})))
    dzf_all = gather(dz_f)
    dz_r, db_r, in_rows, dz2_all, dz1_all = lstm_backward(
        seq(dx_1), w_rev0, None, gate_r, cprev_r, True, 7, dx_f,
        gathers=(('alias', dz2_all, last), ('alias', dz1_all, {'start': (2,), 'end': (3,)})))
    dzr_all = gather(dz_r)
    in_grad = jnp.swapaxes(seq(in_rows), 0, 1)

    db_own = jnp.stack([jnp.sum(d, axis=0) for d in (db_1, db_2, db_f, db_r)])
    db_own, dzr_all = lax.optimization_barrier((db_own, dzr_all))
    db_all = jnp.sum(gather(db_own), axis=0)

    dw_up = weight_grad(all_1, all_2, dz2_all, False, steps, 2, 1)
    dw_up = weight_grad(all_x1, all_1, dz1_all, False, steps, 2, 0, dw_up)
    dw_f = weight_grad(all_x, all_f, dzf_all, False, steps)
    dw_r = weight_grad(all_x, all_r, dzr_all, True, steps)
    return (in_grad, dw_f, db_all[2], dw_r, db_all[3], dw_up, db_all[:2])


def solution(mesh):
    return jax.shard_map(step_grads, mesh=mesh,
                         in_specs=(P(DATA_AXIS), P(DATA_AXIS), P(), P(), P(), P(), P(), P()),
                         out_specs=(P(DATA_AXIS), P(), P(), P(), P(), P(), P()),
                         check_vma=False)
```

time: 1580 us -> 564 us (0.36)
  waiting for transfers between devices: 680 us -> 0.73 us
  Pallas kernels: 0 us -> 532 us
  matrix products: 499 us -> 0 us
  other arithmetic: 255 us -> 3.24 us
  local copies, waits for them, and re-layouts: 79.8 us -> 11.4 us
  blocking collectives: 37.1 us -> 0 us
    psum x1 -> x0, waiting for transfers between devices: 680 us -> none  [reduce_grads(): lax.psum((dw_cat.astype(jnp.bfloat16), db_sum.astype(jnp.bfloat16)), DATA...]
    pallas_call x0 -> x12, Pallas kernels: none -> 532 us  [the longest x8 305 us: call(): pl.pallas_call(kernel, out_shape=outs + [jax.ShapeDtypeStruct(shape, BF16...]
    dot_general x80 -> x0, matrix products: 499 us -> none  [the longest x32 219 us: back_step(): jnp.einsum('bg,hg->bh', dz_bf, w_rec, preferred_element_type=jnp.float32)]
    concatenate x65 -> x0, other arithmetic: 91.4 us -> none  [the longest x64 61.7 us: back_step(): jnp.concatenate([dc_cur * cand_gate * in_gate * (1.0 - in_gate), dc_cur *...]
    another operation x3 -> x1, other arithmetic: 70.4 us -> 0.71 us  [step_grads(): db_own = jnp.stack([jnp.sum(d, axis=0) for d in (db_1, db_2, db_f, db_r)])]
    dynamic_update_slice x96 -> x0, other arithmetic: 46.9 us -> none  [the longest x64 35.8 us: cell_forward(): return lax.scan(cell_step, init_carry, pre_seq, reverse=backwards)[1]]
    convert_element_type x5 -> x0, other arithmetic: 38.7 us -> none  [the longest x4 38.6 us: reduce_grads(): return (summed[0].astype(jnp.float32), summed[1].astype(jnp.float32))]
    psum x1 -> x0, blocking collectives: 37.1 us -> none  [reduce_grads(): lax.psum((dw_cat.astype(jnp.bfloat16), db_sum.astype(jnp.bfloat16)), DATA...]
  transfers between devices with their start and end apart: 1 -> 3, of which waited for: 1 -> 0; matrix products, arithmetic and copies ran while one was open for 1% -> 1% of each run, Pallas kernels for 0% -> 40%
where the time goes in v1:
time: 564 us; the launch traced here: 561 us
  Pallas kernels  532 us (94%)
  between operations  14.4 us (3%)
  local copies, waits for them, and re-layouts  11.4 us (2%)
    pallas_call x8, Pallas kernels, call(): pl.pallas_call(kernel, out_shape=outs + [jax.ShapeDtypeStruct(shape, BF16...  305 us
    pallas_call x4, Pallas kernels, weight_grad(): pl.pallas_call(functools.partial(dw_kernel, backwards, steps, span // ste...  227 us
  transfers between devices with their start and end apart: 3, of which 0 were waited for; matrix products, arithmetic and copies ran while one was open for 1% of the time, Pallas kernels for 40%

profile of v1, /device:TPU:0, one launch (start us, length us, event | category | flops | bytes accessed | tf_op | source)
XLA Modules:
  0.0 561.4 jit_solution(8946514877533190614)
XLA Ops:
  7.2 0.0 all-gather.10.cloned.1.call-start
  7.2 1.7 copy.34
  8.9 1.3 broadcast_in_dim.7.refs_2_
  10.3 1.3 broadcast_in_dim.6.refs_2_
  11.6 1.5 fusion
  13.1 2.0 copy.39
  15.1 24.3 %lstm_fwd.4 = (f32[8,16,4608]{2,1,0:T(8,128)}, f32[8,16,1152]{2,1,0:T(8,128)}, f32[8,16,1152]{2,1,0:T(8,128)}, bf16[128,1152]{1,0:T(8,128)(2,1)}, bf16[16,128,1152]{2,1,0:T(8,128)(2,1)}) custom-call(bf16[128,1152]{1,0:T(8,128)(2,1)} %bitcast.30, bf16[2304,4608]{1,0:T(8,128)(2,1)} %refs_1_.14, f32[1,4608]{1,0:T(1,128)} %broadcast_in_dim.7.refs_2_), custom_call_target="tpu_custom_call" | custom-call | flops 21743271936 | bytes 41943040 | tf_op jit(solution)/shard_map/lstm_fwd/pallas_call | solution.py:219
  39.4 24.7 %lstm_fwd.5 = (f32[8,16,4608]{2,1,0:T(8,128)}, f32[8,16,1152]{2,1,0:T(8,128)}, f32[8,16,1152]{2,1,0:T(8,128)}, bf16[128,1152]{1,0:T(8,128)(2,1)}, bf16[128,1152]...) custom-call(bf16[128,1152]{1,0:T(8,128)(2,1)} %bitcast.31, ...), custom_call_target="tpu_custom_call", output_to_operand_aliasing={{5}: (5, {})} | custom-call | flops 21743271936 | bytes 41943040 | tf_op jit(solution)/shard_map/lstm_fwd/pallas_call | solution.py:219
  64.2 30.1 %lstm_fwd.6 = (f32[8,16,4608]{2,1,0:T(8,128)}, f32[8,16,1152]{2,1,0:T(8,128)}, f32[8,16,1152]{2,1,0:T(8,128)}, bf16[128,1152]{1,0:T(8,128)(2,1)}, bf16[16,128,11...) custom-call(bf16[128,1152]{1,0:T(8,128)(2,1)} %get-tuple-element.60., ...), custom_call_target="tpu_custom_call", output_to_operand_aliasing={{4}: (4, {}), {5}: (5, {})} | custom-call | flops 21743271936 | bytes 41943040 | tf_op jit(solution)/shard_map/lstm_fwd/pallas_call | solution.py:219
  94.3 33.9 %lstm_fwd.7 = (f32[8,16,4608]{2,1,0:T(8,128)}, f32[8,16,1152]{2,1,0:T(8,128)}, f32[8,16,1152]{2,1,0:T(8,128)}, bf16[128,1152]{1,0:T(8,128)(2,1)}, bf16[16,128,11...) custom-call(bf16[128,1152]{1,0:T(8,128)(2,1)} %get-tuple-element.64., ...), custom_call_target="tpu_custom_call", output_to_operand_aliasing={{4}: (3, {}), {5}: (4, {}), {6}: (5, {})} | custom-call | flops 21743271936 | bytes 41943040 | tf_op jit(solution)/shard_map/lstm_fwd/pallas_call | solution.py:219
  128.1 40.7 %lstm_bwd.4 = (bf16[128,4608]{1,0:T(8,128)(2,1)}, f32[8,4608]{1,0:T(8,128)}, f32[128,1152]{1,0:T(8,128)}, bf16[16,128,1152]{2,1,0:T(8,128)(2,1)}, bf16[16,128,11...) custom-call(f32[8,16,1152]{2,1,0:T(8,128)} %bitcast.27, ...), custom_call_target="tpu_custom_call", output_to_operand_aliasing={{3}: (5, {}), {4}: (6, {}), {5}: (7, {})} | custom-call | flops 32614907904 | bytes 41943040 | tf_op jit(solution)/shard_map/lstm_bwd/pallas_call | solution.py:219
  168.8 34.8 %lstm_bwd.5 = (bf16[128,4608]{1,0:T(8,128)(2,1)}, f32[8,4608]{1,0:T(8,128)}, f32[128,1152]{1,0:T(8,128)}, bf16[16,128,1152]{2,1,0:T(8,128)(2,1)}, bf16[16,128,11...) custom-call(f32[8,16,1152]{2,1,0:T(8,128)} %bitcast.41, ...), custom_call_target="tpu_custom_call", output_to_operand_aliasing={{3}: (5, {}), {4}: (6, {})} | custom-call | flops 32614907904 | bytes 41943040 | tf_op jit(solution)/shard_map/lstm_bwd/pallas_call | solution.py:219
  203.7 67.5 %lstm_bwd.6 = (bf16[128,4608]{1,0:T(8,128)(2,1)}, f32[8,4608]{1,0:T(8,128)}, f32[128,1152]{1,0:T(8,128)}, bf16[16,128,4608]{2,1,0:T(8,128)(2,1)}, bf16[16,128,4608]{2,1,0:T(8,128)(2,1)}) custom-call(f32[8,16,1152]{2,1,0:T(8,128)} %bitcast.39, bf16[2304,4608]{1,0:T(8,128)(2,1)} %refs_1_.14, ...), custom_call_target="tpu_custom_call", output_to_operand_aliasing={{3}: (5, {})} | custom-call | flops 32614907904 | bytes 41943040 | tf_op jit(solution)/shard_map/lstm_bwd/pallas_call | solution.py:219
  271.2 0.0 copy-start.2
  271.2 0.0 copy-start.1
  271.2 0.0 copy-start
  271.2 48.7 %lstm_bwd.7 = (bf16[128,4608]{1,0:T(8,128)(2,1)}, f32[8,4608]{1,0:T(8,128)}, f32[128,1152]{1,0:T(8,128)}, bf16[16,128,4608]{2,1,0:T(8,128)(2,1)}, bf16[16,128,4608]{2,1,0:T(8,128)(2,1)}) custom-call(f32[8,16,1152]{2,1,0:T(8,128)} %bitcast.40, bf16[2304,4608]{1,0:T(8,128)(2,1)} %refs_1_.15, ...), custom_call_target="tpu_custom_call", output_to_operand_aliasing={{3}: (5, {}), {4}: (6, {})} | custom-call | flops 32614907904 | bytes 41943040 | tf_op jit(solution)/shard_map/lstm_bwd/pallas_call | solution.py:219
  319.9 0.0 all-gather.10.cloned.1.call-update
  319.9 0.0 all-gather.8.cloned.1.call-start
  320.0 0.7 all-gather.8.cloned.1.call-update
  320.7 0.0 all-gather.12.cloned.1.call-start
  320.7 1.0 reduce_sum.48
  321.7 0.0 copy-done.2
  321.8 0.0 copy-done.1
  321.9 0.0 copy-done
  321.9 2.1 copy.38
  324.0 0.7 pad_maximum_fusion
  324.7 56.8 %dw.6.refs_0_ = f32[2,2304,4608]{2,1,0:T(8,128)} custom-call(bf16[2048,1152]{1,0:T(8,128)(2,1)} %bitcast.24, bf16[2048,1152]{1,0:T(8,128)(2,1)} %bitcast.35, bf16[2048,4608]{1,0:T(8,128)(2,1)} %bitcast.33), custom_call_target="tpu_custom_call" | custom-call | flops 43486543872 | bytes 94371840 | tf_op jit(solution)/shard_map/dw/pallas_call | solution.py:399
  381.5 56.6 %dw.7 = f32[2,2304,4608]{2,1,0:T(8,128)} custom-call(bf16[2048,1152]{1,0:T(8,128)(2,1)} %bitcast.23, bf16[2048,1152]{1,0:T(8,128)(2,1)} %bitcast.25, bf16[2048,4608]{1,0:T(8,128)(2,1)} %bitcast.22, f32[2,2304,4608]{2,1,0:T(8,128)} %dw.6.refs_0_), custom_call_target="tpu_custom_call", output_to_operand_aliasing={{}: (3, {})} | custom-call | flops 43486543872 | bytes 94371840 | tf_op jit(solution)/shard_map/dw/pallas_call | solution.py:399
  438.1 0.0 all-gather.10.cloned.1.call-done
  438.1 0.0 all-gather.12.cloned.1.call-update
  438.1 56.9 %dw.5 = f32[2304,4608]{1,0:T(8,128)} custom-call(bf16[2048,1152]{1,0:T(8,128)(2,1)} %bitcast.37, bf16[2048,1152]{1,0:T(8,128)(2,1)} %bitcast.34, bf16[2048,4608]{1,0:T(8,128)(2,1)} %all-gather.10.cloned.1.call-done), custom_call_target="tpu_custom_call" | custom-call | flops 43486543872 | bytes 94371840 | tf_op jit(solution)/shard_map/dw/pallas_call | solution.py:399
  495.0 0.0 all-gather.8.cloned.1.call-done.dz_ref
  495.0 56.6 %dw.4 = f32[2304,4608]{1,0:T(8,128)} custom-call(bf16[2048,1152]{1,0:T(8,128)(2,1)} %bitcast.38, bf16[2048,1152]{1,0:T(8,128)(2,1)} %bitcast.36, bf16[2048,4608]{1,0:T(8,128)(2,1)} %all-gather.8.cloned.1.call-done.dz_ref), custom_call_target="tpu_custom_call" | custom-call | flops 43486543872 | bytes 94371840 | tf_op jit(solution)/shard_map/dw/pallas_call | solution.py:399
  551.6 0.0 all-gather.12.cloned.1.call-done
  551.6 1.5 reduce_sum.49
  553.0 0.7 slice_reduce_fusion
  553.7 0.6 slice.22
  (7 shorter events, 0.2 us)
Async XLA Ops:
  7.2 430.9 %all-gather.10.cloned.1.call-start = ((), (), s32[]{:S(2)}) async-start(), calls=%async_computation.1 | async-start | bytes 20054016 | tf_op jit(solution)/shard_map/all_gather | solution.py:415
  271.2 50.5 %copy-start.2 = (f32[8,4608]{1,0:T(8,128)S(1)}, f32[8,4608]{1,0:T(8,128)}, u32[]{:S(2)}) copy-start(f32[8,4608]{1,0:T(8,128)} %get-tuple-element.96) | copy-start | bytes 442372
  271.2 50.6 %copy-start.1 = (f32[8,4608]{1,0:T(8,128)S(1)}, f32[8,4608]{1,0:T(8,128)}, u32[]{:S(2)}) copy-start(f32[8,4608]{1,0:T(8,128)} %get-tuple-element.94) | copy-start | bytes 442372
  271.2 50.7 %copy-start = (f32[8,4608]{1,0:T(8,128)S(1)}, f32[8,4608]{1,0:T(8,128)}, u32[]{:S(2)}) copy-start(f32[8,4608]{1,0:T(8,128)} %get-tuple-element.95) | copy-start | bytes 442372
  319.9 175.1 %all-gather.8.cloned.1.call-start = ((), (), s32[]{:S(2)}) async-start(), calls=%async_computation | async-start | bytes 20054016 | tf_op jit(solution)/shard_map/all_gather | solution.py:415
  320.7 230.9 %all-gather.12.cloned.1.call-start = ((), (), s32[]{:S(2)}) async-start(), calls=%async_computation.2 | async-start | bytes 1253376 | tf_op jit(solution)/shard_map/all_gather | solution.py:415
Sparse Core Ops, SparseCore 0:
  320.0 82.3 all-gather.9
  404.6 82.8 all-gather.7
  489.7 25.6 all-gather.11

commit v2 on v1

--- a/solution.py
+++ b/solution.py
@@ -18,88 +18,98 @@
 
 
 class Exchange:
-    def __init__(self, ref, sems):
-        self.ref, self.sems = ref, sems
-        self.third = ref.shape[2] // 3
+    def __init__(self, ref, sems, fine):
+        self.ref, self.sems, self.fine = ref, sems, fine
+        self.third = ref.shape[-1] // 3
         self.me = lax.axis_index(DATA_AXIS)
-        self.started = []
-
-    def flip(self, dev, bit):
-        return dev + bit * (1 - 2 * ((dev // bit) % 2))
+        self.coord = {bit: (self.me // bit) % 2 for bit in (8, 4, 2, 1)}
+
+    def peer(self, bit):
+        return self.me + bit * (1 - 2 * self.coord[bit])
 
     def bits(self, part):
         return [2 << ((part + r) % 3) for r in range(3)]
 
+    def view(self, at, part=None):
+        index = tuple(pl.ds(0, 2) if at[bit] is None else at[bit] for bit in (8, 4, 2))
+        cols = pl.ds(0, 3 * self.third) if part is None else pl.ds(part * self.third, self.third)
+        return self.ref.at[index + (self.coord[1], slice(None), cols)]
+
     def copies(self, part, rnd):
         bits = self.bits(part)
-        peer = self.flip(self.me, bits[rnd])
+        free = bits[:rnd]
+        picks = [(None,) * rnd]
+        if self.fine and rnd == 2:
+            picks = [(0, 0), (0, 1), (1, 0), (1, 1)]
         out = []
-        for j in range(1 << rnd):
-            blk, got = self.me, peer
-            for k in range(rnd):
-                if (j >> k) & 1:
-                    blk, got = self.flip(blk, bits[k]), self.flip(got, bits[k])
-            out.append((blk, got, peer, part * 7 + (1 << rnd) - 1 + j))
+        for j, pick in enumerate(picks):
+            sent = dict(self.coord)
+            sent.update(zip(free, pick))
+            got = dict(sent)
+            got[bits[rnd]] = 1 - sent[bits[rnd]]
+            slot = part + 3 * rnd if rnd < 2 else 6 + 4 * part + j
+            out.append((self.view(sent, part), self.view(got, part), self.peer(bits[rnd]), slot))
         return out
 
-    def remote(self, blk, cols, peer, slot):
-        view = self.ref.at[blk, :, cols]
+    def remote(self, view, peer, slot):
         return pltpu.make_async_remote_copy(
             src_ref=view, dst_ref=view, send_sem=self.sems.at[0, slot], recv_sem=self.sems.at[1, slot],
             device_id=(peer,), device_id_type=pl.DeviceIdType.MESH)
 
-    def cols(self, part):
-        return pl.ds(part * self.third, self.third)
-
     def each(self, rnd):
-        for part in range(3):
-            for blk, got, peer, slot in self.copies(part, rnd):
-                yield part, blk, got, peer, slot
+        for copies in zip(*[self.copies(part, rnd) for part in range(3)]):
+            yield from copies
 
     def send(self, rnd):
-        for part, blk, got, peer, slot in self.each(rnd):
-            self.remote(blk, self.cols(part), peer, slot).start()
+        for sent, got, peer, slot in self.each(rnd):
+            self.remote(sent, peer, slot).start()
 
     def wait(self, rnd):
-        for part, blk, got, peer, slot in self.each(rnd):
-            self.remote(blk, self.cols(part), peer, slot).wait()
+        for sent, got, peer, slot in self.each(rnd):
+            self.remote(sent, peer, slot).wait()
 
     def own(self):
-        return self.remote(self.me, pl.ds(0, 3 * self.third), self.flip(self.me, 1), 21)
-
-    def share(self, rnd, start):
-        for part, blk, got, peer, slot in self.each(rnd):
-            copy = self.remote(got, self.cols(part), self.flip(self.me, 1), 22 + slot)
+        return self.remote(self.view(self.coord), self.peer(1), 18)
+
+    def share(self, rnd, start, arrived=True):
+        for sent, got, peer, slot in self.each(rnd):
+            if not arrived:
+                self.remote(sent, peer, slot).wait()
+            copy = self.remote(got, self.peer(1), 19 + slot)
             if start:
                 copy.start()
             else:
                 copy.wait()
 
 
-SLOTS = 43
+SLOTS = 37
 
 
 def run_stage(ex, stage, open_ops):
+    arrived = True
     if stage > 0:
         if ('round', stage - 1) in open_ops:
-            ex.wait(stage - 1)
             open_ops.remove(('round', stage - 1))
-        ex.share(stage - 1, True)
-        open_ops.append(('share', stage - 1))
+            arrived = stage < 3
+            if arrived:
+                ex.wait(stage - 1)
     else:
         ex.own().start()
         open_ops.append(('own', 0))
     if stage < 3:
         ex.send(stage)
         open_ops.append(('round', stage))
+    if stage > 0:
+        ex.share(stage - 1, True, arrived)
+        open_ops.append(('share', stage - 1))
 
 
 class Comm:
     def __init__(self, plan, refs, sems, local_sems, sources):
         self.plan = plan
-        self.exs = [Exchange(ref, sems.at[n]) for n, ref in enumerate(refs)]
+        self.exs = [Exchange(ref, sems.at[n], 'fine' in p) for n, (ref, p) in enumerate(zip(refs, plan))]
         self.open_ops = [[] for _ in plan]
-        self.local = [None if src is None else pltpu.make_async_copy(src, ex.ref.at[ex.me], local_sems.at[n])
+        self.local = [None if src is None else pltpu.make_async_copy(src, ex.view(ex.coord), local_sems.at[n])
                       for n, (src, ex) in enumerate(zip(sources, self.exs))]
 
     def begin(self):
@@ -111,8 +121,7 @@
         barrier = pltpu.get_barrier_semaphore()
         ex = self.exs[0]
         for bit in (1, 2, 4, 8):
-            pl.semaphore_signal(barrier, inc=1, device_id=(ex.flip(ex.me, bit),),
-                                device_id_type=pl.DeviceIdType.MESH)
+            pl.semaphore_signal(barrier, inc=1, device_id=(ex.peer(bit),), device_id_type=pl.DeviceIdType.MESH)
         pl.semaphore_wait(barrier, 4)
         for copy in self.local:
             if copy is not None:
@@ -141,7 +150,7 @@
                     ex.own().wait()
 
 
-def fwd_kernel(layer, steps, backwards, with_sum, plan, sources, *refs):
+def fwd_kernel(layer, bias_row, steps, backwards, with_sum, plan, sources, *refs):
     refs = list(refs)
     x_ref, w_hbm, b_ref = refs[:3]
     refs = refs[3:]
@@ -169,7 +178,7 @@
     for gate in range(4):
         w_copy(0, gate).wait()
         cols = pl.ds(gate * hid, hid)
-        pre[:, cols] = jnp.dot(x_ref[...], w_buf[:hid, cols], preferred_element_type=F32) + b_ref[:, cols]
+        pre[:, cols] = jnp.dot(x_ref[...], w_buf[:hid, cols], preferred_element_type=F32) + b_ref[bias_row:bias_row + 1, cols]
 
     def cell(t, z_all, c_prev):
         in_gate = jax.nn.sigmoid(z_all[:, :hid])
@@ -234,18 +243,17 @@
     n_vmem = len(args)
     aliases = {}
     blocks = []
-    devs = lax.axis_size(DATA_AXIS)
     for n, (kind, blk, _) in enumerate(gathers):
         if kind == 'alias':
             aliases[len(args)] = n_outs + n
             args.append(blk)
             blocks.append(blk.shape)
         else:
-            blocks.append((devs,) + (x_rows if kind == 'x' else blk).shape)
+            blocks.append((2, 2, 2, 2) + (x_rows if kind == 'x' else blk).shape)
     return [p for _, _, p in gathers], [kind for kind, _, _ in gathers], blocks, n_vmem, aliases
 
 
-def lstm_forward(x_rows, w_cat, layer, bias_row, steps, backwards, collective, other=None, gathers=()):
+def lstm_forward(x_rows, w_cat, layer, biases, bias_row, steps, backwards, collective, other=None, gathers=()):
     hid = x_rows.shape[1]
     rows = x_rows.shape[0] // steps
     with_sum = other is not None
@@ -253,12 +261,12 @@
             jax.ShapeDtypeStruct((steps, rows, hid), F32),
             jax.ShapeDtypeStruct((steps, rows, hid), F32),
             jax.ShapeDtypeStruct((steps * rows, hid), BF16)]
-    args = [x_rows, w_cat, bias_row]
+    args = [x_rows, w_cat, biases]
     if with_sum:
         outs.append(jax.ShapeDtypeStruct((steps * rows, hid), BF16))
         args.append(other)
     plan, sources, blocks, n_vmem, aliases = gather_args(args, gathers, len(outs), x_rows)
-    return call(functools.partial(fwd_kernel, layer, steps, backwards, with_sum, plan, sources), 'lstm_fwd', args,
+    return call(functools.partial(fwd_kernel, layer, bias_row, steps, backwards, with_sum, plan, sources), 'lstm_fwd', args,
                 n_vmem, outs,
                 [pltpu.VMEM((2 * hid, 4 * hid), BF16), pltpu.VMEM((steps * rows, 4 * hid), F32),
                  pltpu.SemaphoreType.DMA((8,))],
@@ -345,50 +353,62 @@
                 plan, blocks, aliases, collective, 4 * steps * rows * hid * 4 * hid * 12)
 
 
-def dw_kernel(backwards, steps, rows, x_ref, h_ref, dz_ref, *refs):
-    out_ref, shifted, turned = refs[-3:]
+def dw_kernel(backwards, steps, rows, x_hbm, h_hbm, dz_ref, *refs):
+    out_ref, x_buf, h_buf, x_turned, h_turned, x_sems, h_sems = refs[-7:]
     part, col = pl.program_id(0), pl.program_id(1)
     span = steps * rows
-    devs = x_ref.shape[0] // span
-
-    def turn(src):
-        for n in range(devs):
-            at = slice(n * span, (n + 1) * span)
-            turned[:, at] = src[at, :].T
+    devs = x_buf.shape[0] // span
+
+    def copy(src, dst, sems, n):
+        at = pl.ds(pl.multiple_of(n * span, span), span)
+        return pltpu.make_async_copy(src.at[at], dst.at[at], sems.at[n])
 
     @pl.when((part == 0) & (col == 0))
     def _():
-        turn(x_ref)
-
-    @pl.when((part == 1) & (col == 0))
+        for n in range(devs):
+            copy(x_hbm, x_buf, x_sems, n).start()
+        for n in range(devs):
+            copy(h_hbm, h_buf, h_sems, n).start()
+        for n in range(devs):
+            copy(x_hbm, x_buf, x_sems, n).wait()
+            x_turned[:, n * span:(n + 1) * span] = x_buf[n * span:(n + 1) * span, :].T
+
+    @pl.when((part == 0) & (col < devs // 2))
     def _():
-        none = jnp.zeros((rows, h_ref.shape[1]), BF16)
-        for n in range(devs):
-            lo, hi = n * span, (n + 1) * span
+        for half in range(2):
+            copy(h_hbm, h_buf, h_sems, 2 * col + half).wait()
+
+    @pl.when(part == 0)
+    def _():
+        none = jnp.zeros((rows, h_buf.shape[1]), BF16)
+        for half in range(2):
+            first = pl.multiple_of((2 * jnp.minimum(col, devs // 2 - 1) + half) * span, span)
             if backwards:
-                shifted[lo:hi - rows, :] = h_ref[lo + rows:hi, :]
-                shifted[hi - rows:hi, :] = none
+                prev = jnp.concatenate([h_buf[pl.ds(first + rows, span - rows), :], none], axis=0)
             else:
-                shifted[lo + rows:hi, :] = h_ref[lo:hi - rows, :]
-                shifted[lo:lo + rows, :] = none
-        turn(shifted)
-
-    out_ref[...] = jnp.dot(turned[...], dz_ref[...], preferred_element_type=F32)
+                prev = jnp.concatenate([none, h_buf[pl.ds(first, span - rows), :]], axis=0)
+            h_turned[:, pl.ds(first, span)] = prev.T
+        out_ref[...] = jnp.dot(x_turned[...], dz_ref[...], preferred_element_type=F32)
+
+    @pl.when(part == 1)
+    def _():
+        out_ref[...] = jnp.dot(h_turned[...], dz_ref[...], preferred_element_type=F32)
 
 
 def weight_grad(x_all, h_all, dz_all, backwards, steps, planes=None, plane=None, into=None):
-    devs, span, hid = x_all.shape
-    count = devs * span
-    wide = dz_all.shape[2]
+    span, hid = x_all.shape[-2:]
+    count = x_all.size // hid
+    devs = count // span
+    wide = dz_all.shape[-1]
     width = 512
     flat = lambda a: a.reshape(count, a.shape[-1])
     args = [flat(x_all), flat(h_all), flat(dz_all)]
-    whole = pl.BlockSpec((count, hid), lambda p, n: (0, 0), pipeline_mode=pl.Buffered(1))
-    in_specs = [whole, whole, pl.BlockSpec((count, width), lambda p, n: (0, n))]
+    hbm = pl.BlockSpec(memory_space=pl.ANY)
+    in_specs = [hbm, hbm, pl.BlockSpec((count, width), lambda p, n: (0, n))]
     aliases = {}
     if into is not None:
         args.append(into)
-        in_specs.append(pl.BlockSpec(memory_space=pl.ANY))
+        in_specs.append(hbm)
         aliases = {3: 0}
     if planes is None:
         out = jax.ShapeDtypeStruct((2 * hid, wide), F32)
@@ -402,7 +422,8 @@
         out_shape=out,
         in_specs=in_specs,
         out_specs=out_spec,
-        scratch_shapes=[pltpu.VMEM((count, hid), BF16), pltpu.VMEM((hid, count), BF16)],
+        scratch_shapes=[pltpu.VMEM((count, hid), BF16)] * 2 + [pltpu.VMEM((hid, count), BF16)] * 2
+        + [pltpu.SemaphoreType.DMA((devs,))] * 2,
         input_output_aliases=aliases,
         compiler_params=pltpu.CompilerParams(vmem_limit_bytes=VMEM_LIMIT,
                                              dimension_semantics=('arbitrary', 'arbitrary')),
@@ -418,34 +439,36 @@
 def step_grads(inputs, out_grad, w_fwd0, b_fwd0, w_rev0, b_rev0, w_upper, b_upper):
     batch, steps, hid = inputs.shape
     seq = lambda a: a.reshape(steps, batch, a.shape[-1])
-    row = lambda b: b[None, :]
     x_rows = jnp.swapaxes(inputs, 0, 1).reshape(steps * batch, hid)
-    head, tail, last = {'start': (0,), 4: (1,)}, {'start': (2,)}, {'start': (3,)}
+    head, tail, last = {'start': (0,), 1: (1,)}, {'start': (2,)}, {'start': (3,)}
+    late = {'start': (0,), 2: (1,)}
+    b_low = jnp.stack([b_fwd0, b_rev0])
     gate_f, cprev_f, h_f, hb_f, all_x = lstm_forward(
-        x_rows, w_fwd0, None, row(b_fwd0), steps, False, 0, gathers=(('x', None, head),))
-    gate_r, cprev_r, h_r, hb_r, x1, all_x, all_f = lstm_forward(
-        x_rows, w_rev0, None, row(b_rev0), steps, True, 1, h_f, gathers=(('alias', all_x, tail), ('arg', hb_f, head)))
-    gate_1, cprev_1, _, hb_1, all_x, all_f, all_r, all_x1 = lstm_forward(
-        x1, w_upper, 0, row(b_upper[0]), steps, False, 2,
-        gathers=(('alias', all_x, last), ('alias', all_f, tail), ('arg', hb_r, head), ('x', None, head)))
-    gate_2, cprev_2, _, hb_2, all_f, all_r, all_x1, all_1 = lstm_forward(
-        hb_1, w_upper, 1, row(b_upper[1]), steps, False, 3,
-        gathers=(('alias', all_f, last), ('alias', all_r, tail), ('alias', all_x1, tail), ('x', None, head)))
-
-    dz_2, db_2, dx_2, all_r, all_x1, all_1, all_2 = lstm_backward(
+        x_rows, w_fwd0, None, b_low, 0, steps, False, 0, gathers=(('x', None, head),))
+    gate_r, cprev_r, h_r, hb_r, x1, all_f, all_x = lstm_forward(
+        x_rows, w_rev0, None, b_low, 1, steps, True, 1, h_f, gathers=(('arg', hb_f, head), ('alias', all_x, tail)))
+    gate_1, cprev_1, _, hb_1, all_r, all_x1, all_f, all_x = lstm_forward(
+        x1, w_upper, 0, b_upper, 0, steps, False, 2,
+        gathers=(('arg', hb_r, late), ('x', None, late), ('alias', all_f, tail), ('alias', all_x, last)))
+    gate_2, cprev_2, _, hb_2, all_1, all_r, all_x1, all_f = lstm_forward(
+        hb_1, w_upper, 1, b_upper, 1, steps, False, 3,
+        gathers=(('x', None, {'start': (0,)}), ('alias', all_r, tail), ('alias', all_x1, tail),
+                 ('alias', all_f, last)))
+
+    dz_2, db_2, dx_2, all_2, all_1, all_r, all_x1 = lstm_backward(
         jnp.swapaxes(out_grad, 0, 1), w_upper, 1, gate_2, cprev_2, False, 4,
-        gathers=(('alias', all_r, last), ('alias', all_x1, last), ('alias', all_1, tail),
-                 ('arg', hb_2, {'start': (0,), 2: (1,), 5: (2,)})))
-    dz_1, db_1, dx_1, all_1, all_2, dz2_all = lstm_backward(
+        gathers=(('arg', hb_2, {'start': (0,), 2: (1,), 5: (2,)}), ('alias', all_1, {'start': (1,), 2: (2,)}),
+                 ('alias', all_r, last), ('alias', all_x1, last)))
+    dz_1, db_1, dx_1, dz2_all, all_2, all_1 = lstm_backward(
         seq(dx_2), w_upper, 0, gate_1, cprev_1, False, 5,
-        gathers=(('alias', all_1, last), ('alias', all_2, last), ('arg', dz_2, {'start': (0,), 3: (1,)})))
-    dz_f, db_f, dx_f, dz2_all, dz1_all = lstm_backward(
+        gathers=(('arg', dz_2, {'start': (0,), 3: (1,)}), ('alias', all_2, last), ('alias', all_1, last)))
+    dz_f, db_f, dx_f, dz1_all, dz2_all = lstm_backward(
         seq(dx_1), w_fwd0, None, gate_f, cprev_f, False, 6,
-        gathers=(('alias', dz2_all, {'start': (2,)}), ('arg', dz_1, {'start': (0,), 5: (1,)})))
+        gathers=(('arg', dz_1, {'start': (0,), 4: (1,)}), ('alias', dz2_all, tail)))
     dzf_all = gather(dz_f)
-    dz_r, db_r, in_rows, dz2_all, dz1_all = lstm_backward(
+    dz_r, db_r, in_rows, dz1_all, dz2_all = lstm_backward(
         seq(dx_1), w_rev0, None, gate_r, cprev_r, True, 7, dx_f,
-        gathers=(('alias', dz2_all, last), ('alias', dz1_all, {'start': (2,), 'end': (3,)})))
+        gathers=(('alias', dz1_all, {'fine': (), 'start': (2,), 'end': (3,)}), ('alias', dz2_all, last)))
     dzr_all = gather(dz_r)
     in_grad = jnp.swapaxes(seq(in_rows), 0, 1)
 

time: 564 us -> 536 us (0.950)
  Pallas kernels: 532 us -> 506 us
    pallas_call x8, Pallas kernels: 305 us -> 284 us  [call(): pl.pallas_call(kernel, out_shape=outs + [jax.ShapeDtypeStruct(shape, BF16...]
  transfers between devices with their start and end apart: 3 -> 3, of which waited for: 0 -> 0; matrix products, arithmetic and copies ran while one was open for 1% -> 1% of each run, Pallas kernels for 40% -> 42%
where the time goes in v2:
time: 536 us; the launch traced here: 533 us
  Pallas kernels  506 us (94%)
  between operations  14.2 us (3%)
  local copies, waits for them, and re-layouts  8.66 us (2%)
    pallas_call x8, Pallas kernels, call(): pl.pallas_call(kernel, out_shape=outs + [jax.ShapeDtypeStruct(shape, BF16...  284 us
    pallas_call x4, Pallas kernels, weight_grad(): pl.pallas_call(functools.partial(dw_kernel, backwards, steps, span // ste...  221 us
  transfers between devices with their start and end apart: 3, of which 0 were waited for; matrix products, arithmetic and copies ran while one was open for 1% of the time, Pallas kernels for 42%

profile of v2, /device:TPU:0, one launch (start us, length us, event | category | flops | bytes accessed | tf_op | source)
XLA Modules:
  0.0 533.4 jit_solution(4360424034212991318)
XLA Ops:
  7.2 0.0 all-gather.10.cloned.1.call-start
  7.2 1.7 copy.34
  8.9 0.7 stack.24
  9.7 0.7 stack.25
  10.4 2.0 copy.39
  12.4 0.7 pad_maximum_fusion.1.refs_2_
  13.1 21.8 %lstm_fwd.4 = (f32[8,16,4608]{2,1,0:T(8,128)}, f32[8,16,1152]{2,1,0:T(8,128)}, f32[8,16,1152]{2,1,0:T(8,128)}, bf16[128,1152]{1,0:T(8,128)(2,1)}, bf16[2,2,2,2,128,1152]{5,4,3,2,1,0:T(8,128)(2,1)}) custom-call(bf16[128,1152]{1,0:T(8,128)(2,1)} %bitcast.30, bf16[2304,4608]{1,0:T(8,128)(2,1)} %refs_1_.14, f32[2,4608]{1,0:T(2,128)} %pad_maximum_fusion.1.refs_2_), custom_call_target="tpu_custom_call" | custom-call | flops 21743271936 | bytes 41943040 | tf_op jit(solution)/shard_map/lstm_fwd/pallas_call | solution.py:228
  34.9 24.6 %lstm_fwd.5 = (f32[8,16,4608]{2,1,0:T(8,128)}, f32[8,16,1152]{2,1,0:T(8,128)}, f32[8,16,1152]{2,1,0:T(8,128)}, bf16[128,1152]{1,0:T(8,128)(2,1)}, bf16[128,1152]...) custom-call(bf16[128,1152]{1,0:T(8,128)(2,1)} %bitcast.31, ...), custom_call_target="tpu_custom_call", output_to_operand_aliasing={{6}: (5, {})} | custom-call | flops 21743271936 | bytes 41943040 | tf_op jit(solution)/shard_map/lstm_fwd/pallas_call | solution.py:228
  59.5 30.1 %lstm_fwd.6 = (f32[8,16,4608]{2,1,0:T(8,128)}, f32[8,16,1152]{2,1,0:T(8,128)}, f32[8,16,1152]{2,1,0:T(8,128)}, bf16[128,1152]{1,0:T(8,128)(2,1)}, bf16[2,2,2,2,1...) custom-call(bf16[128,1152]{1,0:T(8,128)(2,1)} %get-tuple-element.60., ...), custom_call_target="tpu_custom_call", output_to_operand_aliasing={{6}: (4, {}), {7}: (5, {})} | custom-call | flops 21743271936 | bytes 41943040 | tf_op jit(solution)/shard_map/lstm_fwd/pallas_call | solution.py:228
  89.7 27.5 %lstm_fwd.7 = (f32[8,16,4608]{2,1,0:T(8,128)}, f32[8,16,1152]{2,1,0:T(8,128)}, f32[8,16,1152]{2,1,0:T(8,128)}, bf16[128,1152]{1,0:T(8,128)(2,1)}, bf16[2,2,2,2,1...) custom-call(bf16[128,1152]{1,0:T(8,128)(2,1)} %get-tuple-element.64., ...), custom_call_target="tpu_custom_call", output_to_operand_aliasing={{5}: (3, {}), {6}: (4, {}), {7}: (5, {})} | custom-call | flops 21743271936 | bytes 41943040 | tf_op jit(solution)/shard_map/lstm_fwd/pallas_call | solution.py:228
  117.1 36.0 %lstm_bwd.4 = (bf16[128,4608]{1,0:T(8,128)(2,1)}, f32[8,4608]{1,0:T(8,128)}, f32[128,1152]{1,0:T(8,128)}, bf16[2,2,2,2,128,1152]{5,4,3,2,1,0:T(8,128)(2,1)}, bf1...) custom-call(f32[8,16,1152]{2,1,0:T(8,128)} %bitcast.27, ...), custom_call_target="tpu_custom_call", output_to_operand_aliasing={{4}: (5, {}), {5}: (6, {}), {6}: (7, {})} | custom-call | flops 32614907904 | bytes 41943040 | tf_op jit(solution)/shard_map/lstm_bwd/pallas_call | solution.py:228
  153.1 34.6 %lstm_bwd.5 = (bf16[128,4608]{1,0:T(8,128)(2,1)}, f32[8,4608]{1,0:T(8,128)}, f32[128,1152]{1,0:T(8,128)}, bf16[2,2,2,2,128,4608]{5,4,3,2,1,0:T(8,128)(2,1)}, bf1...) custom-call(f32[8,16,1152]{2,1,0:T(8,128)} %bitcast.41, ...), custom_call_target="tpu_custom_call", output_to_operand_aliasing={{4}: (5, {}), {5}: (6, {})} | custom-call | flops 32614907904 | bytes 41943040 | tf_op jit(solution)/shard_map/lstm_bwd/pallas_call | solution.py:228
  187.7 66.3 %lstm_bwd.6 = (bf16[128,4608]{1,0:T(8,128)(2,1)}, f32[8,4608]{1,0:T(8,128)}, f32[128,1152]{1,0:T(8,128)}, bf16[2,2,2,2,128,4608]{5,4,3,2,1,0:T(8,128)(2,1)}, bf16[2,2,2,2,128,4608]{5,4,3,2,1,0:T(8,128)(2,1)}) custom-call(f32[8,16,1152]{2,1,0:T(8,128)} %bitcast.39, bf16[2304,4608]{1,0:T(8,128)(2,1)} %refs_1_.14, ...), custom_call_target="tpu_custom_call", output_to_operand_aliasing={{4}: (5, {})} | custom-call | flops 32614907904 | bytes 41943040 | tf_op jit(solution)/shard_map/lstm_bwd/pallas_call | solution.py:228
  254.0 0.0 copy-start.2
  254.0 0.0 copy-start.1
  254.0 0.0 copy-start
  254.0 43.5 %lstm_bwd.7 = (bf16[128,4608]{1,0:T(8,128)(2,1)}, f32[8,4608]{1,0:T(8,128)}, f32[128,1152]{1,0:T(8,128)}, bf16[2,2,2,2,128,4608]{5,4,3,2,1,0:T(8,128)(2,1)}, bf16[2,2,2,2,128,4608]{5,4,3,2,1,0:T(8,128)(2,1)}) custom-call(f32[8,16,1152]{2,1,0:T(8,128)} %bitcast.40, bf16[2304,4608]{1,0:T(8,128)(2,1)} %refs_1_.15, ...), custom_call_target="tpu_custom_call", output_to_operand_aliasing={{3}: (5, {}), {4}: (6, {})} | custom-call | flops 32614907904 | bytes 41943040 | tf_op jit(solution)/shard_map/lstm_bwd/pallas_call | solution.py:228
  297.5 0.0 all-gather.10.cloned.1.call-update
  297.5 0.0 all-gather.8.cloned.1.call-start
  297.6 0.7 all-gather.8.cloned.1.call-update
  298.3 0.0 all-gather.12.cloned.1.call-start
  298.3 1.0 reduce_sum.48
  299.3 0.0 copy-done.2
  299.4 0.0 copy-done.1
  299.5 0.0 copy-done
  299.5 2.1 copy.38
  301.6 0.7 pad_maximum_fusion
  302.3 55.2 %dw.6.refs_0_ = f32[2,2304,4608]{2,1,0:T(8,128)} custom-call(bf16[2048,1152]{1,0:T(8,128)(2,1)} %bitcast.24, bf16[2048,1152]{1,0:T(8,128)(2,1)} %bitcast.34, bf16[2048,4608]{1,0:T(8,128)(2,1)} %bitcast.33), custom_call_target="tpu_custom_call" | custom-call | flops 43486543872 | bytes 94371840 | tf_op jit(solution)/shard_map/dw/pallas_call | solution.py:419
  357.6 55.3 %dw.7 = f32[2,2304,4608]{2,1,0:T(8,128)} custom-call(bf16[2048,1152]{1,0:T(8,128)(2,1)} %bitcast.23, bf16[2048,1152]{1,0:T(8,128)(2,1)} %bitcast.25, bf16[2048,4608]{1,0:T(8,128)(2,1)} %bitcast.22, f32[2,2304,4608]{2,1,0:T(8,128)} %dw.6.refs_0_), custom_call_target="tpu_custom_call", output_to_operand_aliasing={{}: (3, {})} | custom-call | flops 43486543872 | bytes 94371840 | tf_op jit(solution)/shard_map/dw/pallas_call | solution.py:419
  412.8 0.0 all-gather.10.cloned.1.call-done
  412.9 0.0 all-gather.12.cloned.1.call-update
  412.9 55.7 %dw.5 = f32[2304,4608]{1,0:T(8,128)} custom-call(bf16[2048,1152]{1,0:T(8,128)(2,1)} %bitcast.37, bf16[2048,1152]{1,0:T(8,128)(2,1)} %bitcast.36, bf16[2048,4608]{1,0:T(8,128)(2,1)} %all-gather.10.cloned.1.call-done), custom_call_target="tpu_custom_call" | custom-call | flops 43486543872 | bytes 94371840 | tf_op jit(solution)/shard_map/dw/pallas_call | solution.py:419
  468.5 0.0 all-gather.8.cloned.1.call-done.dz_ref
  468.6 55.3 %dw.4 = f32[2304,4608]{1,0:T(8,128)} custom-call(bf16[2048,1152]{1,0:T(8,128)(2,1)} %bitcast.38, bf16[2048,1152]{1,0:T(8,128)(2,1)} %bitcast.35, bf16[2048,4608]{1,0:T(8,128)(2,1)} %all-gather.8.cloned.1.call-done.dz_ref), custom_call_target="tpu_custom_call" | custom-call | flops 43486543872 | bytes 94371840 | tf_op jit(solution)/shard_map/dw/pallas_call | solution.py:419
  523.9 0.0 all-gather.12.cloned.1.call-done
  523.9 1.5 reduce_sum.49
  525.3 0.7 slice_reduce_fusion
  526.0 0.6 slice.14
  (7 shorter events, 0.2 us)
Async XLA Ops:
  7.2 405.7 %all-gather.10.cloned.1.call-start = ((), (), s32[]{:S(2)}) async-start(), calls=%async_computation.1 | async-start | bytes 20054016 | tf_op jit(solution)/shard_map/all_gather | solution.py:436
  254.0 45.3 %copy-start.2 = (f32[8,4608]{1,0:T(8,128)S(1)}, f32[8,4608]{1,0:T(8,128)}, u32[]{:S(2)}) copy-start(f32[8,4608]{1,0:T(8,128)} %get-tuple-element.96) | copy-start | bytes 442372
  254.0 45.4 %copy-start.1 = (f32[8,4608]{1,0:T(8,128)S(1)}, f32[8,4608]{1,0:T(8,128)}, u32[]{:S(2)}) copy-start(f32[8,4608]{1,0:T(8,128)} %get-tuple-element.94) | copy-start | bytes 442372
  254.0 45.4 %copy-start = (f32[8,4608]{1,0:T(8,128)S(1)}, f32[8,4608]{1,0:T(8,128)}, u32[]{:S(2)}) copy-start(f32[8,4608]{1,0:T(8,128)} %get-tuple-element.95) | copy-start | bytes 442372
  297.5 171.1 %all-gather.8.cloned.1.call-start = ((), (), s32[]{:S(2)}) async-start(), calls=%async_computation | async-start | bytes 20054016 | tf_op jit(solution)/shard_map/all_gather | solution.py:436
  298.3 225.6 %all-gather.12.cloned.1.call-start = ((), (), s32[]{:S(2)}) async-start(), calls=%async_computation.2 | async-start | bytes 1253376 | tf_op jit(solution)/shard_map/all_gather | solution.py:436
Sparse Core Ops, SparseCore 0:
  297.6 82.2 all-gather.9
  382.2 82.8 all-gather.7
  467.2 25.6 all-gather.11
